TPU v7x, 32 devices: a whole 2x2x4 slice. The times are simulated.
32 devices in a mesh: parts: 2 (over y), section: 2 (over core), tp: 8 (over z, x).
Axes of the slice: x: 2, y: 2, z: 4, core: 2. Of those that a mesh axis runs over, the one named last changes fastest.
Arguments:
- prompt_rows: bfloat16 [128, 8192], P(('parts', 'section', 'tp')), parts along dimension 0, may hold values from -72 to 72
- query_weight: bfloat16 [8192, 8192], P(None, 'tp'), may hold values from -0.0625 to 0.0625
- cache_weight: bfloat16 [8, 8192, 256], P('tp'), may hold values from -1 to 1, as said below
- output_weight: bfloat16 [8192, 8192], P('tp'), may hold values from -0.0625 to 0.0625
- documents: int32 [128], P('parts'), parts along dimension 0, may hold values from 0 to 3, never falling along the last dimension, each value on 1 to 32 neighbouring positions
- page_table: int32 [24], P('parts'), parts along dimension 0, may hold values from 0 to 15, as said below
Outputs:
- branch_output: bfloat16 [128, 8192], P(('parts', 'section', 'tp')), parts along dimension 0
- page_pool: bfloat16 [32, 8, 2048], P(('parts', 'section', 'tp')), parts along dimension 0
There are 2 independent parts, one for each index of `parts`. A program takes and returns all parts, laid end to end along the dimension named above; an argument that names none is the same for every part. Nothing has to cross between parts.
Inputs may be any that keep to these rules, and one draw needn't show every extreme that they name: `cache_weight`: entry t equals entry u whenever t == u. `documents`: ids never fall along the tokens; there are 4 prompts of 1 to 32 tokens, one of exactly 32. `page_table`: entries are distinct pool slots; slot q is owned by the device of index q along section+tp (one slot per device). Entries beyond the number of pages are not used.
All inputs are finite; a program needn't handle non-finite values.
Results may differ from a plain program's by a relative error of at most 0.0085.
The roundings to bfloat16 on the way count: a program that leaves them out, or rounds other values in their place, can miss the bound.
Values may be sent and summed in bfloat16 or wider, within the bound.
No kernel may reach another device: no remote copies, remote signals or barrier semaphores. Data moves between devices by JAX's collectives and lax.ppermute only.
A program may use at most 64 MiB of HBM per device.

v0:
```python
import jax
import jax.numpy as jnp
from jax import lax
from jax.sharding import PartitionSpec as P

KV_HEADS = 8
HEAD = 128
PAGE = 8


rope_base = 500000.0


def from_partner(value, axis, distance):
    mask = 2**distance
    pairs = [(source, source ^ mask) for source in range(lax.axis_size(axis))]
    return lax.ppermute(value, axis, pairs)


def document_layout(documents):
    count = documents.shape[0]
    places = jnp.arange(count, dtype=jnp.int32)
    begins = jnp.concatenate([jnp.ones((1,), dtype=bool), documents[1:] != documents[:-1]])
    firsts = lax.cummax(jnp.where(begins, places, jnp.zeros_like(places)), axis=0)
    offsets = places - firsts
    starts = (offsets % PAGE == 0).astype(jnp.int32)
    pages = jnp.cumsum(starts) - 1
    return (offsets, pages)


def rope_tables(offsets, width):
    half_width = width // 2
    freqs = rope_base ** (-(jnp.arange(half_width, dtype=jnp.float32) * 2.0 / width))
    angles = offsets.astype(jnp.float32)[:, None] * freqs[None, :]
    return (jnp.cos(angles), jnp.sin(angles))


def rotate(values, cosines, sines):
    half_width = values.shape[-1] // 2
    first = values[..., :half_width]
    second = values[..., half_width:]
    return jnp.concatenate(
        [first * cosines - second * sines, second * cosines + first * sines], axis=-1
    )


def finish_cache(keyvals, cosines, sines):
    rotated = rotate(keyvals[:, :HEAD], cosines, sines)
    return jnp.concatenate([rotated, keyvals[:, HEAD:]], axis=1).astype(jnp.bfloat16)


def body(prompt_rows, query_weight, cache_weight, output_weight, documents, page_table):
    tp_count = lax.axis_size("tp")
    owners = lax.axis_size(("section", "tp"))
    section = lax.axis_index("section")
    column = lax.axis_index("tp")
    rows_dev = prompt_rows.shape[0]
    half_rows = rows_dev * tp_count
    total_rows = 2 * half_rows
    query_width = query_weight.shape[1]
    query_heads = query_width // HEAD
    replicas = tp_count // KV_HEADS
    slice_width = HEAD // replicas
    head_weight = cache_weight[0]
    offsets, pages = document_layout(documents)
    cosines, sines = rope_tables(offsets, HEAD)
    own_start = section * half_rows
    own_cos = lax.dynamic_slice_in_dim(cosines, own_start, half_rows, 0)
    own_sin = lax.dynamic_slice_in_dim(sines, own_start, half_rows, 0)
    piece = lax.all_gather(prompt_rows, "tp", axis=0, tiled=True)
    query_rows = jnp.dot(piece, query_weight, preferred_element_type=jnp.float32)
    cache_rows = jnp.dot(piece, head_weight, preferred_element_type=jnp.float32)
    joined = jnp.concatenate([query_rows, cache_rows], axis=1)
    query_part = joined[:, :query_width]
    cache_half = finish_cache(joined[:, query_width:], own_cos, own_sin)
    other = from_partner(cache_half, "section", 0)
    lower = jnp.where(section == 0, cache_half, other)
    upper = jnp.where(section == 0, other, cache_half)
    cache_all = jnp.concatenate([lower, upper], axis=0)
    queries = query_part.reshape(half_rows, query_heads, HEAD)
    queries = rotate(queries, own_cos[:, None, :], own_sin[:, None, :]).astype(jnp.bfloat16)
    keys = cache_all[:, :HEAD]
    values = cache_all[:, HEAD:]
    places = jnp.arange(total_rows, dtype=jnp.int32)
    query_places = own_start + jnp.arange(half_rows, dtype=jnp.int32)
    query_docs = lax.dynamic_slice_in_dim(documents, own_start, half_rows, 0)
    allowed = (query_docs[:, None] == documents[None, :]) & (
        places[None, :] <= query_places[:, None]
    )
    scale = 1.0 / HEAD**0.5
    scores = jnp.einsum("qhd,kd->hqk", queries, keys, preferred_element_type=jnp.float32) * scale
    scores = jnp.where(allowed[None, :, :], scores, -jnp.inf)
    weights = jax.nn.softmax(scores, axis=-1).astype(jnp.bfloat16)
    mixed = jnp.einsum("hqk,kd->qhd", weights, values, preferred_element_type=jnp.float32)
    attention = mixed.astype(jnp.bfloat16).reshape(half_rows, query_heads * HEAD)
    summed = lax.psum_scatter(
        jnp.dot(attention, output_weight, preferred_element_type=jnp.float32),
        "tp",
        scatter_dimension=0,
        tiled=True,
    )
    branch_output = summed.astype(jnp.bfloat16)
    column_start = section * HEAD + column % replicas * slice_width
    share = lax.dynamic_slice_in_dim(cache_all, column_start, slice_width, 1)
    capacity = rows_dev // 4 * PAGE
    row_of = page_table[pages] * PAGE + offsets % PAGE
    outgoing = jnp.zeros((owners * capacity, slice_width), jnp.bfloat16).at[row_of].set(share)
    outgoing = outgoing.reshape(owners, capacity, slice_width)
    arrived = lax.all_to_all(outgoing, ("section", "tp"), split_axis=0, concat_axis=2, tiled=True)
    return (branch_output, arrived)


def solution(mesh):
    return jax.shard_map(
        body,
        mesh=mesh,
        in_specs=(
            P(("parts", "section", "tp"), None),
            P(None, "tp"),
            P("tp", None, None),
            P("tp", None),
            P("parts"),
            P("parts"),
        ),
        out_specs=(P(("parts", "section", "tp"), None), P(("parts", "section", "tp"), None, None)),
        check_vma=False,
    )
```

profile of v0, /device:TPU:0, one launch (start us, length us, event | category | flops | bytes accessed | tf_op | source)
XLA Modules:
  0.0 150.3 jit_solution(4755525236660970167)
XLA Ops:
  0.7 1.8 %fusion.44 = (s32[1]{0:T(128)}, s32[1]{0:T(128)}, s32[1]{0:T(128)}, s32[1]{0:T(128)}, s32[1]{0:T(128)}, /*index=5*/s32[1]{0:T(128)}, s32[1]{0:T(128)}, s32[1]{0:...) fusion(s32[12]{0:T(128)} %param.11), kind=kLoop, calls=%fused_computation.74 | loop fusion | bytes 96 | tf_op jit(solution)/shard_map/gather | solution.py:106
  2.5 0.8 compare_bitcast_fusion
  3.3 0.1 add_select_fusion.1
  3.3 0.1 copy.18
  3.4 0.1 reduce-window.6
  3.6 0.1 reduce-window.9
  3.7 0.2 compare_reduce_fusion.4
  3.9 4.4 %select_reduce_fusion = s32[64]{0:T(128)S(1)} fusion(s32[]{:T(128)} %bitcast.12, s32[]{:T(128)} %bitcast.13, s32[]{:T(128)} %bitcast.14, s32[]{:T(128)} %bitcast.15, s32[]{:T(128)} %bitcast.16, s32[]{:T(128)} %bitcast.18, s32[]{:T(128)} %bitcast.17, s32[64,1]{1,0:T(8,128)S(1)} %reduce-window.9), kind=kLoop, calls=%fused_computation.35 | loop fusion | flops 1024 | bytes 540 | tf_op jit(solution)/shard_map/gather | solution.py:106
  8.3 3.2 %fusion.31 = s32[64,1]{0,1:T(1,128)S(1)} fusion(pred[64]{0:T(512)(128)(4,1)S(1)} %get-tuple-element.8, pred[64]{0:T(512)(128)(4,1)S(1)} %get-tuple-element.5, pred[64]{0:T(512)(128)(4,1)S(1)} %get-tuple-element.6, pred[64]{0:T(512)(128)(4,1)S(1)} %get-tuple-element.7, pred[64]{0:T(512)(128)(4,1)S(1)} %get-tuple-element.4, s32[64]{0:T(128)S(1)} %select_reduce_fusion, ...), kind=kLoop, calls=%fused_computation.63 | loop fusion | flops 384 | bytes 852 | tf_op jit(solution)/shard_map/mul | solution.py:106
  11.5 0.1 copy.22
  11.6 0.1 fusion.15
  11.7 33.3 %all-gather = bf16[8,4,8192]{2,1,0:T(4,128)(2,1)S(1)} all-gather(bf16[1,4,8192]{2,1,0:T(4,128)(2,1)} %bitcast.64), channel_id=1, replica_groups=mesh['parts'=2,'section'=2,'tp'=8] {'tp'}, dimensions={0}, use_global_device_ids=true | all-gather | bytes 589824 | tf_op jit(solution)/shard_map/all_gather | solution.py:70
  45.0 0.1 reshape.264
  45.1 3.0 %fusion.1 = f32[32,256]{1,0:T(8,128)S(1)} fusion(bf16[32,8192]{1,0:T(8,128)(2,1)S(1)} %reshape.264, bf16[1,8192,256]{2,1,0:T(8,128)(2,1)} %param.8), kind=kOutput, calls=%fused_computation.2 | convolution fusion | flops 134217728 | bytes 4751360 | tf_op jit(solution)/shard_map/dot_general | solution.py:72
  48.2 0.1 broadcast_multiply_fusion
  48.2 0.1 subtract_convert_fusion.1
  48.3 0.1 add_convert_fusion.1
  48.4 0.1 pad_maximum_fusion
  48.5 0.7 dynamic_slice.14
  49.2 8.7 %convolution_bitcast_fusion = f32[4,8,8,128]{3,1,2,0:T(8,128)S(1)} fusion(bf16[32,8192]{1,0:T(8,128)(2,1)S(1)} %reshape.264, bf16[8192,1024]{1,0:T(8,128)(2,1)} %param.7), kind=kOutput, calls=%fused_computation.6 | convolution fusion | flops 536870912 | bytes 17432576 | tf_op jit(solution)/shard_map/dot_general | solution.py:71
  58.0 0.1 fusion.43
  58.2 0.1 fusion.26
  58.3 0.6 dynamic-slice
  59.5 0.1 broadcast_select_fusion
  59.6 1.3 scatter_custom_fusion
  60.9 5.8 %all-to-all-start = ((bf16[16,8,128]{2,1,0:T(8,128)(2,1)}), bf16[16,8,128]{2,1,0:T(8,128)(2,1)S(1)}, u32[]{:S(2)}, u32[]{:S(2)}) async-start(bf16[16,8,128]{2,1,0:T(8,128)(2,1)} %bitcast.20), calls=%async_computation | async-start | bytes 65536 | tf_op jit(solution)/shard_map/all_to_all | solution.py:109
  66.7 0.4 fusion.45
  67.2 0.2 fusion.7
  67.4 8.7 %fusion.8 = f32[32,8192]{1,0:T(8,128)S(1)} fusion(bf16[1024,8192]{1,0:T(8,128)(2,1)} %param.9, bf16[8,4,8,128]{3,2,1,0:T(8,128)(2,1)S(1)} %fusion.7), kind=kOutput, calls=%fused_computation.18 | convolution fusion | flops 536870912 | bytes 17891328 | tf_op jit(solution)/shard_map/dot_general | solution.py:97
  76.1 72.9 %all-reduce.2 = bf16[32,8192]{1,0:T(8,128)(2,1)S(1)} all-reduce(f32[32,8192]{1,0:T(8,128)S(1)} %fusion.8), channel_id=2, replica_groups=mesh['parts'=2,'section'=2,'tp'=8] {'tp'}, use_global_device_ids=true, to_apply=%region_3.4.clone | all-reduce | flops 262144 | bytes 1572864
  149.0 0.7 dynamic-slice_convert_fusion
  149.7 0.6 copy.45
  (14 shorter events, 0.2 us)
Async XLA Ops:
  0.6 57.6 %copy-start.1 = (u32[32]{0:T(128)S(1)}, u32[32]{0:T(128)}, u32[]{:S(2)}) copy-start(u32[32]{0:T(128)} %constant.96) | copy-start | bytes 388
  0.6 57.5 %copy-start = (s32[64]{0:T(128)S(1)}, s32[64]{0:T(128)}, u32[]{:S(2)}) copy-start(s32[64]{0:T(128)} %param.10) | copy-start | bytes 772
  48.5 11.0 %collective-permute-start = (bf16[32,256]{1,0:T(8,128)(2,1)S(1)}, bf16[32,256]{1,0:T(8,128)(2,1)S(1)}, u32[]{:S(2)}, u32[]{:S(2)}) collective-permute-start(bf16[32,256]{1,0:T(8,128)(2,1)S(1)} %pad_maximum_fusion), channel_id=1, source_target_pairs={{0,8},{8,0},{1,9},{9,1},{2,10},{10,2},{3,11},{11,3},{4,12},{12,4},... | collective-permute-start | bytes 49160 | tf_op jit(solution)/shard_map/ppermute | solution.py:17
  60.9 88.8 %all-to-all-start = ((bf16[16,8,128]{2,1,0:T(8,128)(2,1)}), bf16[16,8,128]{2,1,0:T(8,128)(2,1)S(1)}, u32[]{:S(2)}, u32[]{:S(2)}) async-start(bf16[16,8,128]{2,1,0:T(8,128)(2,1)} %bitcast.20), calls=%async_computation | async-start | bytes 65536 | tf_op jit(solution)/shard_map/all_to_all | solution.py:109
where the time goes:
time: 151 us; the launch traced here: 150 us
  blocking collectives  106 us (70%)
  matrix products  21.1 us (14%)
  other arithmetic  10.9 us (7%)
  starting transfers between devices  5.83 us (4%)
  local copies, waits for them, and re-layouts  4.85 us (3%)
    unnamed x1, blocking collectives  72.9 us
    all_gather x1, blocking collectives, body(): piece = lax.all_gather(prompt_rows, 'tp', axis=0, tiled=True)  33.3 us
    dot_general x1, matrix products, body(): jnp.dot(attention, output_weight, preferred_element_type=jnp.float32)  8.75 us
    dot_general x1, matrix products, body(): jnp.dot(piece, query_weight, preferred_element_type=jnp.float32)  8.75 us
    all_to_all x1, starting transfers between devices, body(): lax.all_to_all(outgoing, ('section', 'tp'), split_axis=0, concat_axis=2,...  5.82 us
    gather x2, other arithmetic, body(): row_of = page_table[pages] * PAGE + offsets % PAGE  4.6 us
    mul x1, other arithmetic, body(): row_of = page_table[pages] * PAGE + offsets % PAGE  3.23 us
  transfers between devices with their start and end apart: 2, of which 0 were waited for; matrix products, arithmetic and copies ran while one was open for 14% of the time, Pallas kernels for 0%

commit v1 on v0

--- a/solution.py
+++ b/solution.py
@@ -6,25 +6,60 @@
 KV_HEADS = 8
 HEAD = 128
 PAGE = 8
+FEW = 8
 
 
 rope_base = 500000.0
 
 
-def from_partner(value, axis, distance):
-    mask = 2**distance
+def from_partner(value, axis, mask):
     pairs = [(source, source ^ mask) for source in range(lax.axis_size(axis))]
     return lax.ppermute(value, axis, pairs)
+
+
+def few_devices(count):
+    return 4 <= count <= FEW and count & (count - 1) == 0
+
+
+def gather_rows(rows):
+    count = lax.axis_size("tp")
+    if not few_devices(count):
+        return lax.all_gather(rows, "tp", axis=0, tiled=True)
+    column = lax.axis_index("tp")
+    blocks = {0: rows}
+    for mask in range(2, count, 2):
+        blocks[mask] = from_partner(rows, "tp", mask)
+    for mask in range(0, count, 2):
+        blocks[mask + 1] = from_partner(blocks[mask], "tp", 1)
+    stacked = jnp.stack([blocks[mask] for mask in range(count)], axis=0)
+    pieces = []
+    for place in range(count):
+        piece = lax.dynamic_index_in_dim(stacked, place ^ column, 0, keepdims=False)
+        pieces.append(piece)
+    return jnp.concatenate(pieces, axis=0)
+
+
+def scatter_sum(partial, rows_dev):
+    count = lax.axis_size("tp")
+    if not few_devices(count):
+        return lax.psum_scatter(partial, "tp", scatter_dimension=0, tiled=True)
+    column = lax.axis_index("tp")
+    blocks = partial.reshape(count, rows_dev, partial.shape[1])
+    total = lax.dynamic_index_in_dim(blocks, column, 0, keepdims=False)
+    narrow = blocks.astype(jnp.bfloat16)
+    for mask in range(count - 1, 0, -1):
+        sent = lax.dynamic_index_in_dim(narrow, column ^ mask, 0, keepdims=False)
+        total = total + from_partner(sent, "tp", mask).astype(jnp.float32)
+    return total
 
 
 def document_layout(documents):
     count = documents.shape[0]
     places = jnp.arange(count, dtype=jnp.int32)
-    begins = jnp.concatenate([jnp.ones((1,), dtype=bool), documents[1:] != documents[:-1]])
-    firsts = lax.cummax(jnp.where(begins, places, jnp.zeros_like(places)), axis=0)
+    firsts = jnp.sum((documents[None, :] < documents[:, None]).astype(jnp.int32), axis=1)
     offsets = places - firsts
-    starts = (offsets % PAGE == 0).astype(jnp.int32)
-    pages = jnp.cumsum(starts) - 1
+    starts = (offsets % PAGE == 0)[None, :] & (places[None, :] <= places[:, None])
+    pages = jnp.sum(starts.astype(jnp.int32), axis=1) - 1
     return (offsets, pages)
 
 
@@ -67,13 +102,11 @@
     own_start = section * half_rows
     own_cos = lax.dynamic_slice_in_dim(cosines, own_start, half_rows, 0)
     own_sin = lax.dynamic_slice_in_dim(sines, own_start, half_rows, 0)
-    piece = lax.all_gather(prompt_rows, "tp", axis=0, tiled=True)
-    query_rows = jnp.dot(piece, query_weight, preferred_element_type=jnp.float32)
+    piece = gather_rows(prompt_rows)
     cache_rows = jnp.dot(piece, head_weight, preferred_element_type=jnp.float32)
-    joined = jnp.concatenate([query_rows, cache_rows], axis=1)
-    query_part = joined[:, :query_width]
-    cache_half = finish_cache(joined[:, query_width:], own_cos, own_sin)
-    other = from_partner(cache_half, "section", 0)
+    query_part = jnp.dot(piece, query_weight, preferred_element_type=jnp.float32)
+    cache_half = finish_cache(cache_rows, own_cos, own_sin)
+    other = from_partner(cache_half, "section", 1)
     lower = jnp.where(section == 0, cache_half, other)
     upper = jnp.where(section == 0, other, cache_half)
     cache_all = jnp.concatenate([lower, upper], axis=0)
@@ -93,20 +126,20 @@
     weights = jax.nn.softmax(scores, axis=-1).astype(jnp.bfloat16)
     mixed = jnp.einsum("hqk,kd->qhd", weights, values, preferred_element_type=jnp.float32)
     attention = mixed.astype(jnp.bfloat16).reshape(half_rows, query_heads * HEAD)
-    summed = lax.psum_scatter(
-        jnp.dot(attention, output_weight, preferred_element_type=jnp.float32),
-        "tp",
-        scatter_dimension=0,
-        tiled=True,
-    )
-    branch_output = summed.astype(jnp.bfloat16)
     column_start = section * HEAD + column % replicas * slice_width
     share = lax.dynamic_slice_in_dim(cache_all, column_start, slice_width, 1)
     capacity = rows_dev // 4 * PAGE
-    row_of = page_table[pages] * PAGE + offsets % PAGE
-    outgoing = jnp.zeros((owners * capacity, slice_width), jnp.bfloat16).at[row_of].set(share)
+    slots = jnp.arange(page_table.shape[0], dtype=jnp.int32)
+    hit = pages[:, None] == slots[None, :]
+    table_at = jnp.sum(jnp.where(hit, page_table[None, :], 0), axis=1)
+    row_of = table_at * PAGE + offsets % PAGE
+    pool_rows = jnp.arange(owners * capacity, dtype=jnp.int32)
+    placed = (pool_rows[:, None] == row_of[None, :]).astype(jnp.bfloat16)
+    outgoing = jnp.dot(placed, share, preferred_element_type=jnp.float32).astype(jnp.bfloat16)
     outgoing = outgoing.reshape(owners, capacity, slice_width)
     arrived = lax.all_to_all(outgoing, ("section", "tp"), split_axis=0, concat_axis=2, tiled=True)
+    partial = jnp.dot(attention, output_weight, preferred_element_type=jnp.float32)
+    branch_output = scatter_sum(partial, rows_dev).astype(jnp.bfloat16)
     return (branch_output, arrived)
 
 

time: 151 us -> 68 us (0.45)
  blocking collectives: 106 us -> 0 us
  starting transfers between devices: 5.83 us -> 26.7 us
  waiting for transfers between devices: 0.01 us -> 9.11 us
  other arithmetic: 10.9 us -> 3.81 us
    unnamed x1 -> x0, blocking collectives: 72.9 us -> none
    all_gather x1 -> x0, blocking collectives: 33.3 us -> none  [body(): piece = lax.all_gather(prompt_rows, 'tp', axis=0, tiled=True)]
    ppermute x1 -> x15, starting transfers between devices: 0.01 us -> 22 us  [from_partner(): return lax.ppermute(value, axis, pairs)]
    ppermute x1 -> x15, waiting for transfers between devices: 0.01 us -> 9.11 us  [from_partner(): return lax.ppermute(value, axis, pairs)]
    gather x2 -> x0, other arithmetic: 4.6 us -> none  [body(): row_of = page_table[pages] * PAGE + offsets % PAGE]
    mul x1 -> x0, other arithmetic: 3.23 us -> none  [body(): row_of = page_table[pages] * PAGE + offsets % PAGE]
    gather x1 -> x0, local copies, waits for them, and re-layouts: 1.79 us -> none  [body(): row_of = page_table[pages] * PAGE + offsets % PAGE]
    reduce_sum x0 -> x3, other arithmetic: none -> 1.76 us  [the longest x1 0.91 us: document_layout(): jnp.sum((documents[None, :] < documents[:, None]).astype(jnp.int32), axis=1)]
  transfers between devices with their start and end apart: 2 -> 16, of which waited for: 0 -> 7; matrix products, arithmetic and copies ran while one was open for 14% -> 9% of each run, Pallas kernels for 0% -> 0%
where the time goes in v1:
time: 68 us; the launch traced here: 67.6 us
  starting transfers between devices  26.7 us (39%)
  matrix products  22.1 us (32%)
  waiting for transfers between devices  9.11 us (13%)
  local copies, waits for them, and re-layouts  4.95 us (7%)
  other arithmetic  3.81 us (6%)
  between operations  0.92 us (1%)
    ppermute x15, starting transfers between devices, from_partner(): return lax.ppermute(value, axis, pairs)  22 us
    ppermute x15, waiting for transfers between devices, from_partner(): return lax.ppermute(value, axis, pairs)  9.11 us
    dot_general x1, matrix products, body(): jnp.dot(piece, query_weight, preferred_element_type=jnp.float32)  8.76 us
    dot_general x1, matrix products, body(): jnp.dot(attention, output_weight, preferred_element_type=jnp.float32)  8.63 us
    all_to_all x1, starting transfers between devices, body(): lax.all_to_all(outgoing, ('section', 'tp'), split_axis=0, concat_axis=2,...  4.73 us
    dot_general x1, matrix products, body(): cache_rows = jnp.dot(piece, head_weight, preferred_element_type=jnp.float32)  3.01 us
    unnamed x16, local copies, waits for them, and re-layouts  2.34 us
  transfers between devices with their start and end apart: 16, of which 7 were waited for; matrix products, arithmetic and copies ran while one was open for 9% of the time, Pallas kernels for 0%

profile of v1, /device:TPU:0, one launch (start us, length us, event | category | flops | bytes accessed | tf_op | source)
XLA Modules:
  0.0 67.6 jit_solution(11010513600274081855)
XLA Ops:
  0.6 3.1 %collective-permute-start.1 = (bf16[4,8192]{1,0:T(4,128)(2,1)}, bf16[4,8192]{1,0:T(4,128)(2,1)S(1)}, u32[]{:S(2)}, u32[]{:S(2)}) collective-permute-start(bf16[4,8192]{1,0:T(4,128)(2,1)} %param.6), channel_id=1, source_target_pairs={{0,2},{1,3},{2,0},{3,1},{4,6},{5,7},{6,4},{7,5},{8,10},{9,11},{10,... | collective-permute-start | bytes 196616 | tf_op jit(solution)/shard_map/ppermute | solution.py:17
  3.7 1.5 %collective-permute-start = (bf16[4,8192]{1,0:T(4,128)(2,1)}, bf16[4,8192]{1,0:T(4,128)(2,1)S(1)}, u32[]{:S(2)}, u32[]{:S(2)}) collective-permute-start(bf16[4,8192]{1,0:T(4,128)(2,1)} %param.6), channel_id=1, source_target_pairs={{0,1},{1,0},{2,3},{3,2},{4,5},{5,4},{6,7},{7,6},{8,9},{9,8},{10,11... | collective-permute-start | bytes 196616 | tf_op jit(solution)/shard_map/ppermute | solution.py:17
  5.2 2.5 %collective-permute-start.5 = (bf16[4,8192]{1,0:T(4,128)(2,1)}, bf16[4,8192]{1,0:T(4,128)(2,1)S(1)}, u32[]{:S(2)}, u32[]{:S(2)}) collective-permute-start(bf16[4,8192]{1,0:T(4,128)(2,1)} %param.6), channel_id=1, source_target_pairs={{0,6},{1,7},{2,4},{3,5},{4,2},{5,3},{6,0},{7,1},{8,14},{9,15},{10,... | collective-permute-start | bytes 196616 | tf_op jit(solution)/shard_map/ppermute | solution.py:17
  7.8 0.9 %convert_reduce_fusion.1 = s32[64]{0:T(128)S(1)} fusion(s32[64]{0:T(128)} %param.10), kind=kLoop, calls=%fused_computation.63 | loop fusion | flops 12224 | bytes 512 | tf_op jit(solution)/shard_map/reduce_sum | solution.py:59
  8.8 0.9 %bitcast_dynamic-update-slice_fusion.7 = bf16[8,4,8192]{2,1,0:T(4,128)(2,1)S(1)} fusion(bf16[4,8192]{1,0:T(4,128)(2,1)} %param.6), kind=kLoop, calls=%fused_computation.43 | loop fusion | bytes 131072
  9.7 0.7 %dynamic_slice.72 = s32[32]{0:T(128)S(1)} dynamic-slice(s32[64]{0:T(128)} %param.10, s32[]{:T(128)S(6)} %select_n.91), dynamic_slice_sizes={32} | dynamic-slice | bytes 260 | tf_op jit(solution)/shard_map/dynamic_slice | solution.py:119
  10.5 0.7 %select_reduce_fusion = s32[64]{0:T(128)S(1)} fusion(s32[12]{0:T(128)} %param.11, s32[64]{0:T(128)S(1)} %broadcast_add_fusion), kind=kLoop, calls=%fused_computation.81 | loop fusion | flops 2240 | bytes 560 | tf_op jit(solution)/shard_map/reduce_sum | solution.py:134
  11.3 0.7 %fusion.32 = pred[32,64]{1,0:T(8,128)(4,1)S(1)} fusion(s32[32]{0:T(128)S(1)} %iota_add_fusion, s32[64]{0:T(128)} %param.10, s32[32]{0:T(128)S(1)} %dynamic_slice.72), kind=kLoop, calls=%fused_computation.76 | loop fusion | flops 6144 | bytes 2560 | tf_op jit(solution)/shard_map/and | solution.py:120
  12.1 0.6 collective-permute-start.2
  12.7 1.5 %collective-permute-start.6 = (bf16[4,8192]{1,0:T(4,128)(2,1)S(1)}, bf16[4,8192]{1,0:T(4,128)(2,1)S(1)}, u32[]{:S(2)}, u32[]{:S(2)}) collective-permute-start(bf16[4,8192]{1,0:T(4,128)(2,1)S(1)} %collective-permute-done.5), channel_id=1, source_target_pairs={{0,1},{1,0},{2,3},{3,2},{4,5},{5,4},{6,7},{7,6},{8,9},{9,8},{10,11... | collective-permute-start | bytes 196616 | tf_op jit(solution)/shard_map/ppermute | solution.py:17
  14.2 0.6 collective-permute-start.4
  14.9 1.7 %collective-permute-done.2 = bf16[4,8192]{1,0:T(4,128)(2,1)S(1)} collective-permute-done((bf16[4,8192]{1,0:T(4,128)(2,1)S(1)}, bf16[4,8192]{1,0:T(4,128)(2,1)S(1)}, u32[]{:S(2)}, u32[]{:S(2)}) %collective-permute-start.2) | collective-permute-done | bytes 65568 | tf_op jit(solution)/shard_map/ppermute | solution.py:17
  16.7 1.9 %collective-permute-done.4 = bf16[4,8192]{1,0:T(4,128)(2,1)S(1)} collective-permute-done((bf16[4,8192]{1,0:T(4,128)(2,1)S(1)}, bf16[4,8192]{1,0:T(4,128)(2,1)S(1)}, u32[]{:S(2)}, u32[]{:S(2)}) %collective-permute-start.4) | collective-permute-done | bytes 65568 | tf_op jit(solution)/shard_map/ppermute | solution.py:17
  19.3 3.0 %fusion.3 = f32[32,256]{1,0:T(8,128)S(1)} fusion(bf16[32,8192]{1,0:T(8,128)(2,1)S(1)} %concatenate.14, bf16[1,8192,256]{2,1,0:T(8,128)(2,1)} %param.8), kind=kOutput, calls=%fused_computation.3 | convolution fusion | flops 134217728 | bytes 4751360 | tf_op jit(solution)/shard_map/dot_general | solution.py:106
  22.3 8.8 %convolution_bitcast_fusion = f32[4,8,8,128]{3,1,2,0:T(8,128)S(1)} fusion(bf16[32,8192]{1,0:T(8,128)(2,1)S(1)} %concatenate.14, bf16[8192,1024]{1,0:T(8,128)(2,1)} %param.7), kind=kOutput, calls=%fused_computation.7 | convolution fusion | flops 536870912 | bytes 17432576 | tf_op jit(solution)/shard_map/dot_general | solution.py:107
  31.5 1.0 %collective-permute-done.7 = bf16[32,256]{1,0:T(8,128)(2,1)S(1)} collective-permute-done((bf16[32,256]{1,0:T(8,128)(2,1)S(1)}, bf16[32,256]{1,0:T(8,128)(2,1)S(1)}, u32[]{:S(2)}, u32[]{:S(2)}) %collective-permute-start.7) | collective-permute-done | bytes 16416 | tf_op jit(solution)/shard_map/ppermute | solution.py:17
  33.0 0.6 fusion.9
  33.6 8.6 %fusion.72 = (bf16[8,4,8192]{2,0,1:T(8,128)(2,1)S(1)}, f32[8,4,8192]{2,0,1:T(8,128)S(1)}) fusion(bf16[1024,8192]{1,0:T(8,128)(2,1)} %param.9, bf16[8,4,1024]{2,1,0:T(4,128)(2,1)S(1)} %dot_general.24), kind=kOutput, calls=%fused_computation.114 | convolution fusion | flops 537133056 | bytes 18415616 | tf_op jit(solution)/shard_map/dot_general | solution.py:141
  42.3 1.0 %constant_dynamic-slice_fusion.6 = (bf16[1,4,8192]{2,0,1:T(2,128)(2,1)S(1)}, bf16[1,4,8192]{2,0,1:T(2,128)(2,1)S(1)}, bf16[1,4,8192]{2,0,1:T(2,128)(2,1)S(1)}, b...) fusion(bf16[8,4,8192]{2,0,1:T(8,128)(2,1)S(1)} %get-tuple-eleme, ...), kind=kLoop, calls=%fused_computation.89 | loop fusion | bytes 917532 | tf_op jit(solution)/shard_map/jit(dynamic_index_in_dim)/dynamic_slice | solution.py:51
  43.5 2.9 %collective-permute-start.9 = (bf16[4,8192]{1,0:T(4,128)(2,1)S(1)}, bf16[4,8192]{1,0:T(4,128)(2,1)S(1)}, u32[]{:S(2)}, u32[]{:S(2)}) collective-permute-start(bf16[4,8192]{1,0:T(4,128)(2,1)S(1)} %bitcast.129), channel_id=1, source_target_pairs={{0,6},{1,7},{2,4},{3,5},{4,2},{5,3},{6,0},{7,1},{8,14},{9,15},{10,... | collective-permute-start | bytes 196616 | tf_op jit(solution)/shard_map/ppermute | solution.py:17
  46.4 0.5 collective-permute-start.10
  46.9 0.7 %fusion.10 = bf16[16,8,128]{2,1,0:T(8,128)(2,1)} fusion(s32[64]{0:T(128)S(1)} %multiply_add_fusion, s32[]{:T(128)S(6)} %select_n.97, bf16[32,256]{1,0:T(8,128)(2,1)S(1)} %get-tuple-element.27, bf16[32,256]{1,0:T(8,128)(2,1)S(1)} %get-tuple-element.26), kind=kOutput, calls=%fused_computation.14 | convolution fusion | flops 2154496 | bytes 65796 | tf_op jit(solution)/shard_map/dot_general | solution.py:138
  47.6 4.7 %all-to-all-start = ((bf16[16,8,128]{2,1,0:T(8,128)(2,1)}), bf16[16,8,128]{2,1,0:T(8,128)(2,1)S(1)}, u32[]{:S(2)}, u32[]{:S(2)}) async-start(bf16[16,8,128]{2,1,0:T(8,128)(2,1)} %fusion.10), calls=%async_computation | async-start | bytes 65536 | tf_op jit(solution)/shard_map/all_to_all | solution.py:140
  52.9 2.9 %collective-permute-start.11 = (bf16[4,8192]{1,0:T(4,128)(2,1)S(1)}, bf16[4,8192]{1,0:T(4,128)(2,1)S(1)}, u32[]{:S(2)}, u32[]{:S(2)}) collective-permute-start(bf16[4,8192]{1,0:T(4,128)(2,1)S(1)} %bitcast.130), channel_id=1, source_target_pairs={{0,4},{1,5},{2,6},{3,7},{4,0},{5,1},{6,2},{7,3},{8,12},{9,13},{10,... | collective-permute-start | bytes 196616 | tf_op jit(solution)/shard_map/ppermute | solution.py:17
  55.7 2.4 %collective-permute-start.12 = (bf16[4,8192]{1,0:T(4,128)(2,1)S(1)}, bf16[4,8192]{1,0:T(4,128)(2,1)S(1)}, u32[]{:S(2)}, u32[]{:S(2)}) collective-permute-start(bf16[4,8192]{1,0:T(4,128)(2,1)S(1)} %bitcast.128), channel_id=1, source_target_pairs={{0,3},{1,2},{2,1},{3,0},{4,7},{5,6},{6,5},{7,4},{8,11},{9,10},{10,... | collective-permute-start | bytes 196616 | tf_op jit(solution)/shard_map/ppermute | solution.py:17
  58.1 0.6 collective-permute-start.13
  58.7 0.6 collective-permute-start.14
  59.2 2.4 %collective-permute-start.8 = (bf16[4,8192]{1,0:T(4,128)(2,1)S(1)}, bf16[4,8192]{1,0:T(4,128)(2,1)S(1)}, u32[]{:S(2)}, u32[]{:S(2)}) collective-permute-start(bf16[4,8192]{1,0:T(4,128)(2,1)S(1)} %bitcast.124), channel_id=1, source_target_pairs={{0,7},{1,6},{2,5},{3,4},{4,3},{5,2},{6,1},{7,0},{8,15},{9,14},{10,... | collective-permute-start | bytes 196616 | tf_op jit(solution)/shard_map/ppermute | solution.py:17
  61.7 0.4 collective-permute-done.12
  62.9 3.3 %collective-permute-done.8 = bf16[4,8192]{1,0:T(4,128)(2,1)S(1)} collective-permute-done((bf16[4,8192]{1,0:T(4,128)(2,1)S(1)}, bf16[4,8192]{1,0:T(4,128)(2,1)S(1)}, u32[]{:S(2)}, u32[]{:S(2)}) %collective-permute-start.8) | collective-permute-done | bytes 65568 | tf_op jit(solution)/shard_map/ppermute | solution.py:17
  66.2 0.8 %fusion.17 = bf16[4,8192]{1,0:T(4,128)(2,1)} fusion(bf16[4,8192]{1,0:T(4,128)(2,1)S(1)} %collective-permute-done.14, bf16[4,8192]{1,0:T(4,128)(2,1)S(1)} %collective-permute-done.13, bf16[4,8192]{1,0:T(4,128)(2,1)S(1)} %collective-permute-done.12, bf16[4,8192]{1,0:T(4,128)(2,1)S(1)} %collective-permute-done.11, ...), kind=kLoop, calls=%fused_computation.25 | loop fusion | flops 491520 | bytes 655360 | tf_op jit(solution)/shard_map/convert_element_type | solution.py:142
  67.0 0.6 copy.62
  (49 shorter events, 3.7 us)
Async XLA Ops:
  0.6 11.5 %collective-permute-start.1 = (bf16[4,8192]{1,0:T(4,128)(2,1)}, bf16[4,8192]{1,0:T(4,128)(2,1)S(1)}, u32[]{:S(2)}, u32[]{:S(2)}) collective-permute-start(bf16[4,8192]{1,0:T(4,128)(2,1)} %param.6), channel_id=1, source_target_pairs={{0,2},{1,3},{2,0},{3,1},{4,6},{5,7},{6,4},{7,5},{8,10},{9,11},{10,... | collective-permute-start | bytes 196616 | tf_op jit(solution)/shard_map/ppermute | solution.py:17
  3.7 11.1 %collective-permute-start = (bf16[4,8192]{1,0:T(4,128)(2,1)}, bf16[4,8192]{1,0:T(4,128)(2,1)S(1)}, u32[]{:S(2)}, u32[]{:S(2)}) collective-permute-start(bf16[4,8192]{1,0:T(4,128)(2,1)} %param.6), channel_id=1, source_target_pairs={{0,1},{1,0},{2,3},{3,2},{4,5},{5,4},{6,7},{7,6},{8,9},{9,8},{10,11... | collective-permute-start | bytes 196616 | tf_op jit(solution)/shard_map/ppermute | solution.py:17
  5.2 7.5 %collective-permute-start.5 = (bf16[4,8192]{1,0:T(4,128)(2,1)}, bf16[4,8192]{1,0:T(4,128)(2,1)S(1)}, u32[]{:S(2)}, u32[]{:S(2)}) collective-permute-start(bf16[4,8192]{1,0:T(4,128)(2,1)} %param.6), channel_id=1, source_target_pairs={{0,6},{1,7},{2,4},{3,5},{4,2},{5,3},{6,0},{7,1},{8,14},{9,15},{10,... | collective-permute-start | bytes 196616 | tf_op jit(solution)/shard_map/ppermute | solution.py:17
  7.7 6.5 %collective-permute-start.3 = (bf16[4,8192]{1,0:T(4,128)(2,1)}, bf16[4,8192]{1,0:T(4,128)(2,1)S(1)}, u32[]{:S(2)}, u32[]{:S(2)}) collective-permute-start(bf16[4,8192]{1,0:T(4,128)(2,1)} %param.6), channel_id=1, source_target_pairs={{0,4},{1,5},{2,6},{3,7},{4,0},{5,1},{6,2},{7,3},{8,12},{9,13},{10,... | collective-permute-start | bytes 196616 | tf_op jit(solution)/shard_map/ppermute | solution.py:17
  12.1 4.5 %collective-permute-start.2 = (bf16[4,8192]{1,0:T(4,128)(2,1)S(1)}, bf16[4,8192]{1,0:T(4,128)(2,1)S(1)}, u32[]{:S(2)}, u32[]{:S(2)}) collective-permute-start(bf16[4,8192]{1,0:T(4,128)(2,1)S(1)} %collective-permute-done.1), channel_id=1, source_target_pairs={{0,1},{1,0},{2,3},{3,2},{4,5},{5,4},{6,7},{7,6},{8,9},{9,8},{10,11... | collective-permute-start | bytes 196616 | tf_op jit(solution)/shard_map/ppermute | solution.py:17
  12.7 5.9 %collective-permute-start.6 = (bf16[4,8192]{1,0:T(4,128)(2,1)S(1)}, bf16[4,8192]{1,0:T(4,128)(2,1)S(1)}, u32[]{:S(2)}, u32[]{:S(2)}) collective-permute-start(bf16[4,8192]{1,0:T(4,128)(2,1)S(1)} %collective-permute-done.5), channel_id=1, source_target_pairs={{0,1},{1,0},{2,3},{3,2},{4,5},{5,4},{6,7},{7,6},{8,9},{9,8},{10,11... | collective-permute-start | bytes 196616 | tf_op jit(solution)/shard_map/ppermute | solution.py:17
  14.2 4.3 %collective-permute-start.4 = (bf16[4,8192]{1,0:T(4,128)(2,1)S(1)}, bf16[4,8192]{1,0:T(4,128)(2,1)S(1)}, u32[]{:S(2)}, u32[]{:S(2)}) collective-permute-start(bf16[4,8192]{1,0:T(4,128)(2,1)S(1)} %collective-permute-done.3), channel_id=1, source_target_pairs={{0,1},{1,0},{2,3},{3,2},{4,5},{5,4},{6,7},{7,6},{8,9},{9,8},{10,11... | collective-permute-start | bytes 196616 | tf_op jit(solution)/shard_map/ppermute | solution.py:17
  31.3 1.2 %collective-permute-start.7 = (bf16[32,256]{1,0:T(8,128)(2,1)S(1)}, bf16[32,256]{1,0:T(8,128)(2,1)S(1)}, u32[]{:S(2)}, u32[]{:S(2)}) collective-permute-start(bf16[32,256]{1,0:T(8,128)(2,1)S(1)} %pad_maximum_fusion), channel_id=1, source_target_pairs={{0,8},{8,0},{1,9},{9,1},{2,10},{10,2},{3,11},{11,3},{4,12},{12,4},... | collective-permute-start | bytes 49160 | tf_op jit(solution)/shard_map/ppermute | solution.py:17
  43.5 15.2 %collective-permute-start.9 = (bf16[4,8192]{1,0:T(4,128)(2,1)S(1)}, bf16[4,8192]{1,0:T(4,128)(2,1)S(1)}, u32[]{:S(2)}, u32[]{:S(2)}) collective-permute-start(bf16[4,8192]{1,0:T(4,128)(2,1)S(1)} %bitcast.129), channel_id=1, source_target_pairs={{0,6},{1,7},{2,4},{3,5},{4,2},{5,3},{6,0},{7,1},{8,14},{9,15},{10,... | collective-permute-start | bytes 196616 | tf_op jit(solution)/shard_map/ppermute | solution.py:17
  46.4 12.8 %collective-permute-start.10 = (bf16[4,8192]{1,0:T(4,128)(2,1)S(1)}, bf16[4,8192]{1,0:T(4,128)(2,1)S(1)}, u32[]{:S(2)}, u32[]{:S(2)}) collective-permute-start(bf16[4,8192]{1,0:T(4,128)(2,1)S(1)} %bitcast.126), channel_id=1, source_target_pairs={{0,5},{1,4},{2,7},{3,6},{4,1},{5,0},{6,3},{7,2},{8,13},{9,12},{10,... | collective-permute-start | bytes 196616 | tf_op jit(solution)/shard_map/ppermute | solution.py:17
  47.6 14.1 %all-to-all-start = ((bf16[16,8,128]{2,1,0:T(8,128)(2,1)}), bf16[16,8,128]{2,1,0:T(8,128)(2,1)S(1)}, u32[]{:S(2)}, u32[]{:S(2)}) async-start(bf16[16,8,128]{2,1,0:T(8,128)(2,1)} %fusion.10), calls=%async_computation | async-start | bytes 65536 | tf_op jit(solution)/shard_map/all_to_all | solution.py:140
  52.9 8.9 %collective-permute-start.11 = (bf16[4,8192]{1,0:T(4,128)(2,1)S(1)}, bf16[4,8192]{1,0:T(4,128)(2,1)S(1)}, u32[]{:S(2)}, u32[]{:S(2)}) collective-permute-start(bf16[4,8192]{1,0:T(4,128)(2,1)S(1)} %bitcast.130), channel_id=1, source_target_pairs={{0,4},{1,5},{2,6},{3,7},{4,0},{5,1},{6,2},{7,3},{8,12},{9,13},{10,... | collective-permute-start | bytes 196616 | tf_op jit(solution)/shard_map/ppermute | solution.py:17
  55.7 6.4 %collective-permute-start.12 = (bf16[4,8192]{1,0:T(4,128)(2,1)S(1)}, bf16[4,8192]{1,0:T(4,128)(2,1)S(1)}, u32[]{:S(2)}, u32[]{:S(2)}) collective-permute-start(bf16[4,8192]{1,0:T(4,128)(2,1)S(1)} %bitcast.128), channel_id=1, source_target_pairs={{0,3},{1,2},{2,1},{3,0},{4,7},{5,6},{6,5},{7,4},{8,11},{9,10},{10,... | collective-permute-start | bytes 196616 | tf_op jit(solution)/shard_map/ppermute | solution.py:17
  58.1 4.4 %collective-permute-start.13 = (bf16[4,8192]{1,0:T(4,128)(2,1)S(1)}, bf16[4,8192]{1,0:T(4,128)(2,1)S(1)}, u32[]{:S(2)}, u32[]{:S(2)}) collective-permute-start(bf16[4,8192]{1,0:T(4,128)(2,1)S(1)} %bitcast.127), channel_id=1, source_target_pairs={{0,2},{1,3},{2,0},{3,1},{4,6},{5,7},{6,4},{7,5},{8,10},{9,11},{10,... | collective-permute-start | bytes 196616 | tf_op jit(solution)/shard_map/ppermute | solution.py:17
  58.7 4.3 %collective-permute-start.14 = (bf16[4,8192]{1,0:T(4,128)(2,1)S(1)}, bf16[4,8192]{1,0:T(4,128)(2,1)S(1)}, u32[]{:S(2)}, u32[]{:S(2)}) collective-permute-start(bf16[4,8192]{1,0:T(4,128)(2,1)S(1)} %bitcast.125), channel_id=1, source_target_pairs={{0,1},{1,0},{2,3},{3,2},{4,5},{5,4},{6,7},{7,6},{8,9},{9,8},{10,11... | collective-permute-start | bytes 196616 | tf_op jit(solution)/shard_map/ppermute | solution.py:17
  59.2 7.0 %collective-permute-start.8 = (bf16[4,8192]{1,0:T(4,128)(2,1)S(1)}, bf16[4,8192]{1,0:T(4,128)(2,1)S(1)}, u32[]{:S(2)}, u32[]{:S(2)}) collective-permute-start(bf16[4,8192]{1,0:T(4,128)(2,1)S(1)} %bitcast.124), channel_id=1, source_target_pairs={{0,7},{1,6},{2,5},{3,4},{4,3},{5,2},{6,1},{7,0},{8,15},{9,14},{10,... | collective-permute-start | bytes 196616 | tf_op jit(solution)/shard_map/ppermute | solution.py:17

commit v2 on v1

--- a/solution.py
+++ b/solution.py
@@ -1,12 +1,20 @@
+import functools
+
 import jax
 import jax.numpy as jnp
+import numpy as np
 from jax import lax
+from jax.experimental import pallas as pl
+from jax.experimental.pallas import tpu as pltpu
 from jax.sharding import PartitionSpec as P
 
 KV_HEADS = 8
 HEAD = 128
 PAGE = 8
 FEW = 8
+VM = pl.BlockSpec(memory_space=pltpu.VMEM)
+SM = pl.BlockSpec(memory_space=pltpu.SMEM)
+ANY = pl.BlockSpec(memory_space=pl.ANY)
 
 
 rope_base = 500000.0
@@ -15,42 +23,6 @@
 def from_partner(value, axis, mask):
     pairs = [(source, source ^ mask) for source in range(lax.axis_size(axis))]
     return lax.ppermute(value, axis, pairs)
-
-
-def few_devices(count):
-    return 4 <= count <= FEW and count & (count - 1) == 0
-
-
-def gather_rows(rows):
-    count = lax.axis_size("tp")
-    if not few_devices(count):
-        return lax.all_gather(rows, "tp", axis=0, tiled=True)
-    column = lax.axis_index("tp")
-    blocks = {0: rows}
-    for mask in range(2, count, 2):
-        blocks[mask] = from_partner(rows, "tp", mask)
-    for mask in range(0, count, 2):
-        blocks[mask + 1] = from_partner(blocks[mask], "tp", 1)
-    stacked = jnp.stack([blocks[mask] for mask in range(count)], axis=0)
-    pieces = []
-    for place in range(count):
-        piece = lax.dynamic_index_in_dim(stacked, place ^ column, 0, keepdims=False)
-        pieces.append(piece)
-    return jnp.concatenate(pieces, axis=0)
-
-
-def scatter_sum(partial, rows_dev):
-    count = lax.axis_size("tp")
-    if not few_devices(count):
-        return lax.psum_scatter(partial, "tp", scatter_dimension=0, tiled=True)
-    column = lax.axis_index("tp")
-    blocks = partial.reshape(count, rows_dev, partial.shape[1])
-    total = lax.dynamic_index_in_dim(blocks, column, 0, keepdims=False)
-    narrow = blocks.astype(jnp.bfloat16)
-    for mask in range(count - 1, 0, -1):
-        sent = lax.dynamic_index_in_dim(narrow, column ^ mask, 0, keepdims=False)
-        total = total + from_partner(sent, "tp", mask).astype(jnp.float32)
-    return total
 
 
 def document_layout(documents):
@@ -84,7 +56,7 @@
     return jnp.concatenate([rotated, keyvals[:, HEAD:]], axis=1).astype(jnp.bfloat16)
 
 
-def body(prompt_rows, query_weight, cache_weight, output_weight, documents, page_table):
+def body_many(prompt_rows, query_weight, cache_weight, output_weight, documents, page_table):
     tp_count = lax.axis_size("tp")
     owners = lax.axis_size(("section", "tp"))
     section = lax.axis_index("section")
@@ -102,7 +74,7 @@
     own_start = section * half_rows
     own_cos = lax.dynamic_slice_in_dim(cosines, own_start, half_rows, 0)
     own_sin = lax.dynamic_slice_in_dim(sines, own_start, half_rows, 0)
-    piece = gather_rows(prompt_rows)
+    piece = lax.all_gather(prompt_rows, "tp", axis=0, tiled=True)
     cache_rows = jnp.dot(piece, head_weight, preferred_element_type=jnp.float32)
     query_part = jnp.dot(piece, query_weight, preferred_element_type=jnp.float32)
     cache_half = finish_cache(cache_rows, own_cos, own_sin)
@@ -139,13 +111,309 @@
     outgoing = outgoing.reshape(owners, capacity, slice_width)
     arrived = lax.all_to_all(outgoing, ("section", "tp"), split_axis=0, concat_axis=2, tiled=True)
     partial = jnp.dot(attention, output_weight, preferred_element_type=jnp.float32)
-    branch_output = scatter_sum(partial, rows_dev).astype(jnp.bfloat16)
-    return (branch_output, arrived)
+    summed = lax.psum_scatter(partial, "tp", scatter_dimension=0, tiled=True)
+    return (summed.astype(jnp.bfloat16), arrived)
+
+
+def stream(count, rows, source, target, sems):
+    return [
+        pltpu.make_async_copy(
+            source.at[pl.ds(i * rows, rows), :], target.at[pl.ds(i * rows, rows), :], sems.at[i]
+        )
+        for i in range(count)
+    ]
+
+
+def layout_kernel(
+    rows_dev, capacity, place_ref, docs_ref, table_ref, freq_ref, cos_ref, sin_ref, allow_ref, put_ref
+):
+    section, column = place_ref[0], place_ref[1]
+    total = docs_ref.shape[1]
+    half = total // 2
+    i32 = jnp.int32
+    sub = lax.broadcasted_iota(i32, (total, total), 0)
+    lane = lax.broadcasted_iota(i32, (total, total), 1)
+    eye = sub == lane
+
+    def token_of(place):
+        within = place % half
+        return place // half * half + (within // rows_dev ^ column) * rows_dev + within % rows_dev
+
+    def to_column(row):
+        return jnp.sum(jnp.where(eye, row, 0), axis=1, keepdims=True)
+
+    def to_row(col):
+        return jnp.sum(jnp.where(eye, col, 0), axis=0, keepdims=True)
+
+    doc_row = docs_ref[...]
+    doc_col = to_column(doc_row)
+    first = jnp.sum((doc_row < doc_col).astype(i32), axis=1, keepdims=True)
+    token_col = lax.broadcasted_iota(i32, (total, 1), 0)
+    off_col = token_col - first
+    off_row = to_row(off_col)
+    begins = (off_row % PAGE == 0) & (lane <= sub)
+    page_col = jnp.sum(begins.astype(i32), axis=1, keepdims=True) - 1
+    slots = lax.broadcasted_iota(i32, (total, table_ref.shape[1]), 1)
+    slot_col = jnp.sum(jnp.where(slots == page_col, table_ref[...], 0), axis=1, keepdims=True)
+    row_col = slot_col * PAGE + off_col % PAGE
+    by_place = lane == token_of(sub)
+    place_off = jnp.sum(jnp.where(by_place, off_row, 0), axis=1, keepdims=True)
+    place_doc = jnp.sum(jnp.where(by_place, doc_row, 0), axis=1, keepdims=True)
+    to_place = sub == token_of(lane)
+    place_doc_row = jnp.sum(jnp.where(to_place, doc_col, 0), axis=0, keepdims=True)
+    place_row_row = jnp.sum(jnp.where(to_place, row_col, 0), axis=0, keepdims=True)
+    upper = section == 1
+    own_doc = jnp.where(upper, place_doc[half:], place_doc[:half])
+    own_off = jnp.where(upper, place_off[half:], place_off[:half])
+    own_token = token_of(section * half + lax.broadcasted_iota(i32, (half, total), 0))
+    key_token = token_of(lax.broadcasted_iota(i32, (half, total), 1))
+    allow = (own_doc == place_doc_row) & (key_token <= own_token)
+    allow_ref[...] = allow.astype(jnp.float32)
+    angle = own_off.astype(jnp.float32) * freq_ref[...]
+    cos_ref[...] = jnp.cos(angle)
+    lanes = lax.broadcasted_iota(i32, angle.shape, 1)
+    sines = jnp.sin(angle)
+    sin_ref[...] = jnp.where(lanes < HEAD // 2, -sines, sines)
+    tp_count = half // rows_dev
+    out_rows = tp_count * capacity
+    out_sub = lax.broadcasted_iota(i32, (out_rows, total), 0)
+    owner = section * tp_count + (out_sub // capacity ^ column)
+    wanted = owner * capacity + out_sub % capacity
+    put_ref[...] = (wanted == place_row_row).astype(jnp.bfloat16)
+
+
+def turn(values, cosines, sines):
+    return values * cosines + pltpu.roll(values, HEAD // 2, 1) * sines
+
+
+def cache_kernel(
+    count, *refs
+):
+    blocks, (weight, cos_ref, sin_ref, rows_ref, cache_ref, held, sems) = refs[:count], refs[count:]
+    depth = weight.shape[0]
+    chunks = sems.shape[0]
+    step = depth // chunks
+    copies = stream(chunks, step, weight, held, sems)
+    for copy in copies:
+        copy.start()
+    rows_dev = blocks[0].shape[0]
+    pair = max(1, 8 // rows_dev)
+    for m in range(0, count, pair):
+        joined = jnp.concatenate([blocks[m + j][...].astype(jnp.float32) for j in range(pair)], axis=0)
+        rows_ref[pl.ds(m * rows_dev, pair * rows_dev), :] = joined.astype(jnp.bfloat16)
+    total = jnp.zeros(cache_ref.shape, jnp.float32)
+    for i, copy in enumerate(copies):
+        copy.wait()
+        total += jnp.dot(
+            rows_ref[:, i * step : (i + 1) * step],
+            held[i * step : (i + 1) * step, :],
+            preferred_element_type=jnp.float32,
+        )
+    cache_ref[:, :HEAD] = turn(total[:, :HEAD], cos_ref[...], sin_ref[...]).astype(jnp.bfloat16)
+    cache_ref[:, HEAD:] = total[:, HEAD:].astype(jnp.bfloat16)
+
+
+def query_kernel(rows_ref, weight, cos_ref, sin_ref, query_ref, held, sems):
+    depth = weight.shape[0]
+    chunks = sems.shape[0]
+    step = depth // chunks
+    copies = stream(chunks, step, weight, held, sems)
+    for copy in copies:
+        copy.start()
+    total = jnp.zeros(query_ref.shape, jnp.float32)
+    for i, copy in enumerate(copies):
+        copy.wait()
+        total += jnp.dot(
+            rows_ref[:, i * step : (i + 1) * step],
+            held[i * step : (i + 1) * step, :],
+            preferred_element_type=jnp.float32,
+        )
+    for h in range(query_ref.shape[1] // HEAD):
+        at = slice(h * HEAD, (h + 1) * HEAD)
+        query_ref[:, at] = turn(total[:, at], cos_ref[...], sin_ref[...]).astype(jnp.bfloat16)
+
+
+def output_kernel(
+    count, place_ref, query_ref, own_ref, other_ref, allow_ref, put_ref, weight, *rest
+):
+    outs, own_out, own_cache, (held, sems) = rest[: count - 1], rest[count - 1], rest[count], rest[count + 1 :]
+    chunks = sems.shape[0]
+    width = weight.shape[1]
+    step = width // chunks
+    copies = [
+        pltpu.make_async_copy(
+            weight.at[:, pl.ds(i * step, step)], held.at[:, pl.ds(i * step, step)], sems.at[i]
+        )
+        for i in range(chunks)
+    ]
+    for copy in copies:
+        copy.start()
+    half = query_ref.shape[0]
+    rows_dev = half // count
+    heads = query_ref.shape[1] // HEAD
+    first = place_ref[0] == 0
+    own, other = own_ref[...], other_ref[...]
+    cache = jnp.concatenate([jnp.where(first, own, other), jnp.where(first, other, own)], axis=0)
+    keys, values = cache[:, :HEAD], cache[:, HEAD:]
+    allow = allow_ref[...] > 0.5
+    mixed = []
+    for h in range(heads):
+        query = query_ref[:, h * HEAD : (h + 1) * HEAD]
+        scores = lax.dot_general(
+            query, keys, (((1,), (1,)), ((), ())), preferred_element_type=jnp.float32
+        )
+        scores = jnp.where(allow, scores * (1.0 / HEAD**0.5), -jnp.inf)
+        top = jnp.max(scores, axis=1, keepdims=True)
+        raised = jnp.exp(scores - top)
+        weights = (raised / jnp.sum(raised, axis=1, keepdims=True)).astype(jnp.bfloat16)
+        mixed.append(jnp.dot(weights, values, preferred_element_type=jnp.float32).astype(jnp.bfloat16))
+    attention = jnp.concatenate(mixed, axis=1)
+    placed = jnp.dot(put_ref[...], cache, preferred_element_type=jnp.float32)
+    capacity = put_ref.shape[0] // count
+    wide = 2 * HEAD
+    own_cache[...] = placed[:capacity].astype(jnp.bfloat16)
+    for m in range(1, count):
+        mine = placed[m * capacity : (m + 1) * capacity].astype(jnp.bfloat16)
+        for part in range(capacity // rows_dev):
+            outs[m - 1][:, width + part * wide : width + (part + 1) * wide] = mine[
+                part * rows_dev : (part + 1) * rows_dev
+            ]
+    for i, copy in enumerate(copies):
+        copy.wait()
+        at = slice(i * step, (i + 1) * step)
+        part = jnp.dot(attention, held[:, at], preferred_element_type=jnp.float32)
+        own_out[:, at] = part[:rows_dev]
+        for m in range(1, count):
+            outs[m - 1][:, at] = part[m * rows_dev : (m + 1) * rows_dev].astype(jnp.bfloat16)
+
+
+def finish_kernel(count, place_ref, *rest):
+    got, (own_out, own_cache, branch_ref, pool_ref) = rest[: count - 1], rest[count - 1 :]
+    column = place_ref[1]
+    rows_dev, width = own_out.shape
+    capacity = own_cache.shape[0]
+    wide = 2 * HEAD
+    total = own_out[...]
+    for block in got:
+        total += block[:, :width].astype(jnp.float32)
+    branch_ref[...] = total.astype(jnp.bfloat16)
+    for m in range(count):
+        if m == 0:
+            cache = own_cache[...]
+        else:
+            cache = jnp.concatenate(
+                [
+                    got[m - 1][:, width + part * wide : width + (part + 1) * wide].astype(jnp.float32)
+                    for part in range(capacity // rows_dev)
+                ],
+                axis=0,
+            ).astype(jnp.bfloat16)
+        head = column ^ m
+        pool_ref[0, :, pl.ds(pl.multiple_of(head * HEAD, HEAD), HEAD)] = cache[:, :HEAD]
+        pool_ref[0, :, pl.ds(pl.multiple_of((count + head) * HEAD, HEAD), HEAD)] = cache[:, HEAD:]
+
+
+def params(mib):
+    return pltpu.CompilerParams(vmem_limit_bytes=mib << 20)
+
+
+def cost(flops, read):
+    return pl.CostEstimate(flops=flops, bytes_accessed=read, transcendentals=0)
+
+
+def body_few(prompt_rows, query_weight, cache_weight, output_weight, documents, page_table):
+    count = lax.axis_size("tp")
+    section = lax.axis_index("section")
+    column = lax.axis_index("tp")
+    rows_dev, depth = prompt_rows.shape
+    half = rows_dev * count
+    total = 2 * half
+    query_width = query_weight.shape[1]
+    out_width = output_weight.shape[1]
+    capacity = rows_dev // 4 * PAGE
+    bf16, f32 = jnp.bfloat16, jnp.float32
+    shape = jax.ShapeDtypeStruct
+    place = jnp.stack([section, column]).astype(jnp.int32)
+    bands = np.float64(rope_base) ** (-(np.arange(HEAD // 2) * 2.0 / HEAD))
+    freqs = jnp.asarray(np.concatenate([bands, bands])[None, :], f32)
+
+    blocks = {0: prompt_rows}
+    for mask in range(2, count, 2):
+        blocks[mask] = from_partner(prompt_rows, "tp", mask)
+    for mask in range(0, count, 2):
+        blocks[mask + 1] = from_partner(blocks[mask], "tp", 1)
+
+    cosines, sines, allow, put = pl.pallas_call(
+        functools.partial(layout_kernel, rows_dev, capacity),
+        out_shape=(
+            shape((half, HEAD), f32),
+            shape((half, HEAD), f32),
+            shape((half, total), f32),
+            shape((count * capacity, total), bf16),
+        ),
+        in_specs=[SM, VM, VM, VM],
+        out_specs=(VM, VM, VM, VM),
+        compiler_params=params(4),
+        name="layout",
+    )(place, documents[None, :], page_table[None, :], freqs)
+
+    rows, cache = pl.pallas_call(
+        functools.partial(cache_kernel, count),
+        out_shape=(shape((half, depth), bf16), shape((half, 2 * HEAD), bf16)),
+        in_specs=[VM] * count + [ANY, VM, VM],
+        out_specs=(VM, VM),
+        scratch_shapes=[pltpu.VMEM((depth, 2 * HEAD), bf16), pltpu.SemaphoreType.DMA((4,))],
+        compiler_params=params(8),
+        cost_estimate=cost(2 * half * depth * 2 * HEAD, depth * 4 * HEAD),
+        name="cache",
+    )(*[blocks[m] for m in range(count)], cache_weight[0], cosines, sines)
+
+    other = from_partner(cache, "section", 1)
+
+    queries = pl.pallas_call(
+        query_kernel,
+        out_shape=shape((half, query_width), bf16),
+        in_specs=[VM, ANY, VM, VM],
+        out_specs=VM,
+        scratch_shapes=[pltpu.VMEM((depth, query_width), bf16), pltpu.SemaphoreType.DMA((16,))],
+        compiler_params=params(24),
+        cost_estimate=cost(2 * half * depth * query_width, 2 * depth * query_width),
+        name="query",
+    )(rows, query_weight, cosines, sines)
+
+    spare = capacity // rows_dev * 2 * HEAD
+    sent = pl.pallas_call(
+        functools.partial(output_kernel, count),
+        out_shape=tuple(shape((rows_dev, out_width + spare), bf16) for _ in range(count - 1))
+        + (shape((rows_dev, out_width), f32), shape((capacity, 2 * HEAD), bf16)),
+        in_specs=[SM, VM, VM, VM, VM, VM, ANY],
+        out_specs=(VM,) * (count + 1),
+        scratch_shapes=[pltpu.VMEM((query_width, out_width), bf16), pltpu.SemaphoreType.DMA((16,))],
+        compiler_params=params(24),
+        cost_estimate=cost(2 * half * out_width * query_width, 2 * out_width * query_width),
+        name="output",
+    )(place, queries, cache, other, allow, put, output_weight)
+
+    got = [None] * (count - 1)
+    for mask in range(count - 1, 0, -1):
+        got[mask - 1] = from_partner(sent[mask - 1], "tp", mask)
+
+    branch, pool = pl.pallas_call(
+        functools.partial(finish_kernel, count),
+        out_shape=(shape((rows_dev, out_width), bf16), shape((1, capacity, 2 * count * HEAD), bf16)),
+        in_specs=[SM] + [VM] * (count + 1),
+        out_specs=(VM, VM),
+        compiler_params=params(8),
+        name="finish",
+    )(place, *got, sent[count - 1], sent[count])
+    return (branch, pool)
 
 
 def solution(mesh):
+    count = mesh.shape["tp"]
+    few = count == KV_HEADS and count <= FEW and count & (count - 1) == 0
     return jax.shard_map(
-        body,
+        body_few if few else body_many,
         mesh=mesh,
         in_specs=(
             P(("parts", "section", "tp"), None),

time: 68 us -> 61.3 us (0.901)
  matrix products: 22.1 us -> 0 us
  Pallas kernels: 0 us -> 18.8 us
  local copies, waits for them, and re-layouts: 4.95 us -> 10.8 us
  starting transfers between devices: 26.7 us -> 22.9 us
  other arithmetic: 3.81 us -> 0.07 us
  waiting for transfers between devices: 9.11 us -> 7.77 us
    dot_general x5 -> x0, matrix products: 21.7 us -> none  [the longest x1 8.76 us: body(): jnp.dot(piece, query_weight, preferred_element_type=jnp.float32)]
    pallas_call x0 -> x5, Pallas kernels: none -> 18.8 us  [the longest x1 10.1 us: body_few(): pl.pallas_call(functools.partial(output_kernel, count), out_shape=tuple((...]
    unnamed x16 -> x14, local copies, waits for them, and re-layouts: 2.34 us -> 10.8 us
    all_to_all x1 -> x0, starting transfers between devices: 4.73 us -> none  [body(): lax.all_to_all(outgoing, ('section', 'tp'), split_axis=0, concat_axis=2,...]
    dynamic_slice x3 -> x0, local copies, waits for them, and re-layouts: 1.86 us -> none  [the longest x1 1.04 us: scatter_sum(): sent = lax.dynamic_index_in_dim(narrow, column ^ mask, 0, keepdims=False)]
    reduce_sum x3 -> x0, other arithmetic: 1.76 us -> none  [the longest x1 0.91 us: document_layout(): jnp.sum((documents[None, :] < documents[:, None]).astype(jnp.int32), axis=1)]
    ppermute x15, waiting for transfers between devices: 9.11 us -> 7.77 us  [from_partner(): return lax.ppermute(value, axis, pairs)]
    ppermute x15, starting transfers between devices: 22 us -> 22.9 us  [from_partner(): return lax.ppermute(value, axis, pairs)]
  transfers between devices with their start and end apart: 16 -> 15, of which waited for: 7 -> 3; matrix products, arithmetic and copies ran while one was open for 9% -> 0% of each run, Pallas kernels for 0% -> 9%
where the time goes in v2:
time: 61.3 us; the launch traced here: 61 us
  starting transfers between devices  22.9 us (37%)
  Pallas kernels  18.8 us (31%)
  local copies, waits for them, and re-layouts  10.8 us (18%)
  waiting for transfers between devices  7.77 us (13%)
  between operations  0.75 us (1%)
    ppermute x15, starting transfers between devices, from_partner(): return lax.ppermute(value, axis, pairs)  22.9 us
    unnamed x14, local copies, waits for them, and re-layouts  10.8 us
    pallas_call x1, Pallas kernels, body_few(): pl.pallas_call(functools.partial(output_kernel, count), out_shape=tuple((...  10.1 us
    ppermute x15, waiting for transfers between devices, from_partner(): return lax.ppermute(value, axis, pairs)  7.77 us
    pallas_call x1, Pallas kernels, body_few(): pl.pallas_call(query_kernel, out_shape=shape((half, query_width), bf16),...  4.52 us
    pallas_call x1, Pallas kernels, body_few(): pl.pallas_call(functools.partial(cache_kernel, count), out_shape=(shape((...  1.91 us
    pallas_call x1, Pallas kernels, body_few(): pl.pallas_call(functools.partial(finish_kernel, count), out_shape=(shape(...  1.27 us
  transfers between devices with their start and end apart: 15, of which 3 were waited for; matrix products, arithmetic and copies ran while one was open for 0% of the time, Pallas kernels for 9%

profile of v2, /device:TPU:0, one launch (start us, length us, event | category | flops | bytes accessed | tf_op | source)
XLA Modules:
  0.0 61.0 jit_solution(9848222104851310795)
XLA Ops:
  0.6 4.1 %collective-permute-start.3 = (bf16[4,8192]{1,0:T(4,128)(2,1)}, bf16[4,8192]{1,0:T(4,128)(2,1)S(1)}, u32[]{:S(2)}, u32[]{:S(2)}) collective-permute-start(bf16[4,8192]{1,0:T(4,128)(2,1)} %refs_0_.1), channel_id=1, source_target_pairs={{0,4},{1,5},{2,6},{3,7},{4,0},{5,1},{6,2},{7,3},{8,12},{9,13},{10,... | collective-permute-start | bytes 196616 | tf_op jit(solution)/shard_map/ppermute | solution.py:25
  4.8 1.6 %collective-permute-start.1 = (bf16[4,8192]{1,0:T(4,128)(2,1)}, bf16[4,8192]{1,0:T(4,128)(2,1)S(1)}, u32[]{:S(2)}, u32[]{:S(2)}) collective-permute-start(bf16[4,8192]{1,0:T(4,128)(2,1)} %refs_0_.1), channel_id=1, source_target_pairs={{0,2},{1,3},{2,0},{3,1},{4,6},{5,7},{6,4},{7,5},{8,10},{9,11},{10,... | collective-permute-start | bytes 196616 | tf_op jit(solution)/shard_map/ppermute | solution.py:25
  6.3 0.0 collective-permute-start.5
  6.3 1.7 %collective-permute-start = (bf16[4,8192]{1,0:T(4,128)(2,1)}, bf16[4,8192]{1,0:T(4,128)(2,1)S(1)}, u32[]{:S(2)}, u32[]{:S(2)}) collective-permute-start(bf16[4,8192]{1,0:T(4,128)(2,1)} %refs_0_.1), channel_id=1, source_target_pairs={{0,1},{1,0},{2,3},{3,2},{4,5},{5,4},{6,7},{7,6},{8,9},{9,8},{10,11... | collective-permute-start | bytes 196616 | tf_op jit(solution)/shard_map/ppermute | solution.py:25
  8.1 2.3 %collective-permute-start.4 = (bf16[4,8192]{1,0:T(4,128)(2,1)S(1)}, bf16[4,8192]{1,0:T(4,128)(2,1)S(1)}, u32[]{:S(2)}, u32[]{:S(2)}) collective-permute-start(bf16[4,8192]{1,0:T(4,128)(2,1)S(1)} %collective-permute-done.3.refs_4_), channel_id=1, source_target_pairs={{0,1},{1,0},{2,3},{3,2},{4,5},{5,4},{6,7},{7,6},{8,9},{9,8},{10,11... | collective-permute-start | bytes 196616 | tf_op jit(solution)/shard_map/ppermute | solution.py:25
  10.4 0.0 collective-permute-done.1.refs_2_
  10.4 0.4 collective-permute-start.2
  10.7 1.9 %collective-permute-done.5.refs_6_ = bf16[4,8192]{1,0:T(4,128)(2,1)S(1)} collective-permute-done((bf16[4,8192]{1,0:T(4,128)(2,1)}, bf16[4,8192]{1,0:T(4,128)(2,1)S(1)}, u32[]{:S(2)}, u32[]{:S(2)}) %collective-permute-start.5) | collective-permute-done | bytes 65568 | tf_op jit(solution)/shard_map/ppermute | solution.py:25
  12.6 1.5 %collective-permute-start.6 = (bf16[4,8192]{1,0:T(4,128)(2,1)S(1)}, bf16[4,8192]{1,0:T(4,128)(2,1)S(1)}, u32[]{:S(2)}, u32[]{:S(2)}) collective-permute-start(bf16[4,8192]{1,0:T(4,128)(2,1)S(1)} %collective-permute-done.5.refs_6_), channel_id=1, source_target_pairs={{0,1},{1,0},{2,3},{3,2},{4,5},{5,4},{6,7},{7,6},{8,9},{9,8},{10,11... | collective-permute-start | bytes 196616 | tf_op jit(solution)/shard_map/ppermute | solution.py:25
  14.1 0.1 pad_add_fusion.place_ref
  14.2 0.7 %copy-done.4 = s32[64]{0:T(128)S(1)} copy-done((s32[64]{0:T(128)S(1)}, s32[64]{0:T(128)}, u32[]{:S(2)}) %copy-start.4) | copy-done | bytes 280
  14.8 0.7 %copy-done.5 = s32[12]{0:T(128)S(1)} copy-done((s32[12]{0:T(128)S(1)}, s32[12]{0:T(128)}, u32[]{:S(2)}) %copy-start.5) | copy-done | bytes 72
  15.5 0.7 %copy-done.6 = f32[1,128]{1,0:T(1,128)S(1)} copy-done((f32[1,128]{1,0:T(1,128)S(1)}, f32[1,128]{1,0:T(1,128)}, u32[]{:S(2)}) %copy-start.6) | copy-done | bytes 536
  16.1 1.0 %layout.1 = (f32[32,128]{1,0:T(8,128)S(1)}, f32[32,128]{1,0:T(8,128)S(1)}, f32[32,64]{1,0:T(8,128)S(1)}, bf16[64,64]{1,0:T(8,128)(2,1)S(1)}) custom-call(s32[2]{0:T(128)S(1)} %pad_add_fusion.place_ref, s32[1,64]{1,0:T(1,128)S(1)} %bitcast.6, s32[1,12]{1,0:T(1,128)S(1)} %bitcast.7, f32[1,128]{1,0:T(1,128)S(1)} %copy-done.6), custom_call_target="tpu_custom_call" | custom-call | tf_op jit(solution)/shard_map/layout/pallas_call | solution.py:346
  17.2 0.0 copy-start.2
  17.2 2.2 %copy-done.2 = bf16[1,8192,256]{2,1,0:T(8,128)(2,1)S(1)} copy-done((bf16[1,8192,256]{2,1,0:T(8,128)(2,1)S(1)}, bf16[1,8192,256]{2,1,0:T(8,128)(2,1)}, u32[]{:S(2)}) %copy-start.2) | copy-done | bytes 4194328
  19.4 0.8 %copy-done.3 = bf16[4,8192]{1,0:T(4,128)(2,1)S(1)} copy-done((bf16[4,8192]{1,0:T(4,128)(2,1)S(1)}, bf16[4,8192]{1,0:T(4,128)(2,1)}, u32[]{:S(2)}) %copy-start.3) | copy-done | bytes 65560
  20.2 1.9 %cache.1 = (bf16[32,8192]{1,0:T(8,128)(2,1)S(1)}, bf16[32,256]{1,0:T(8,128)(2,1)S(1)}) custom-call(bf16[4,8192]{1,0:T(4,128)(2,1)S(1)} %copy-done.3, bf16[4,8192]{1,0:T(4,128)(2,1)S(1)} %collective-permute-done.refs_1_, bf16[4,8192]{1,0:T(4,128)(2,1)S(1)} %collective-permute-done.1.refs_2_, bf16[4,8192]{1,0:T(4,128)(2,1)S(1)} %collective-permute-done.2.refs_3_, ...), custom_call_target="tpu_custom_call" | custom-call | flops 134217728 | bytes 4194304 | tf_op jit(solution)/shard_map/cache/pallas_call | solution.py:360
  22.1 0.1 collective-permute-start.7
  22.2 0.0 copy-start.1
  22.2 5.8 %copy-done.1 = bf16[8192,1024]{1,0:T(8,128)(2,1)S(1)} copy-done((bf16[8192,1024]{1,0:T(8,128)(2,1)S(1)}, bf16[8192,1024]{1,0:T(8,128)(2,1)}, u32[]{:S(2)}) %copy-start.1) | copy-done | bytes 16777240
  28.0 4.5 %query.1.query_ref = bf16[32,1024]{1,0:T(8,128)(2,1)S(1)} custom-call(bf16[32,8192]{1,0:T(8,128)(2,1)S(1)} %get-tuple-element.19.rows_ref, bf16[8192,1024]{1,0:T(8,128)(2,1)S(1)} %copy-done.1, f32[32,128]{1,0:T(8,128)S(1)} %get-tuple-element.17.refs_9_.cos_ref, f32[32,128]{1,0:T(8,128)S(1)} %get-tuple-element.18.refs_10_.sin_ref), custom_call_target="tpu_custom_call" | custom-call | flops 536870912 | bytes 16777216 | tf_op jit(solution)/shard_map/query/pallas_call | solution.py:373
  32.5 10.1 %output.1 = (bf16[4,8704]{1,0:T(4,128)(2,1)S(1)}, bf16[4,8704]{1,0:T(4,128)(2,1)S(1)}, bf16[4,8704]{1,0:T(4,128)(2,1)S(1)}, bf16[4,8704]{1,0:T(4,128)(2,1)S(1)},...) custom-call(s32[2]{0:T(128)S(1)} %pad_add_fusion.place_ref, ...), custom_call_target="tpu_custom_call" | custom-call | flops 536870912 | bytes 16777216 | tf_op jit(solution)/shard_map/output/pallas_call | solution.py:385
  42.7 1.3 %collective-permute-start.8 = (bf16[4,8704]{1,0:T(4,128)(2,1)S(1)}, bf16[4,8704]{1,0:T(4,128)(2,1)S(1)}, u32[]{:S(2)}, u32[]{:S(2)}) collective-permute-start(bf16[4,8704]{1,0:T(4,128)(2,1)S(1)} %get-tuple-element.23), channel_id=1, source_target_pairs={{0,1},{1,0},{2,3},{3,2},{4,5},{5,4},{6,7},{7,6},{8,9},{9,8},{10,11... | collective-permute-start | bytes 208904 | tf_op jit(solution)/shard_map/ppermute | solution.py:25
  43.9 2.3 %collective-permute-start.10 = (bf16[4,8704]{1,0:T(4,128)(2,1)S(1)}, bf16[4,8704]{1,0:T(4,128)(2,1)S(1)}, u32[]{:S(2)}, u32[]{:S(2)}) collective-permute-start(bf16[4,8704]{1,0:T(4,128)(2,1)S(1)} %get-tuple-element.25), channel_id=1, source_target_pairs={{0,3},{1,2},{2,1},{3,0},{4,7},{5,6},{6,5},{7,4},{8,11},{9,10},{10,... | collective-permute-start | bytes 208904 | tf_op jit(solution)/shard_map/ppermute | solution.py:25
  46.2 1.3 %collective-permute-start.11 = (bf16[4,8704]{1,0:T(4,128)(2,1)S(1)}, bf16[4,8704]{1,0:T(4,128)(2,1)S(1)}, u32[]{:S(2)}, u32[]{:S(2)}) collective-permute-start(bf16[4,8704]{1,0:T(4,128)(2,1)S(1)} %get-tuple-element.26), channel_id=1, source_target_pairs={{0,4},{1,5},{2,6},{3,7},{4,0},{5,1},{6,2},{7,3},{8,12},{9,13},{10,... | collective-permute-start | bytes 208904 | tf_op jit(solution)/shard_map/ppermute | solution.py:25
  47.5 2.2 %collective-permute-start.12 = (bf16[4,8704]{1,0:T(4,128)(2,1)S(1)}, bf16[4,8704]{1,0:T(4,128)(2,1)S(1)}, u32[]{:S(2)}, u32[]{:S(2)}) collective-permute-start(bf16[4,8704]{1,0:T(4,128)(2,1)S(1)} %get-tuple-element.27), channel_id=1, source_target_pairs={{0,5},{1,4},{2,7},{3,6},{4,1},{5,0},{6,3},{7,2},{8,13},{9,12},{10,... | collective-permute-start | bytes 208904 | tf_op jit(solution)/shard_map/ppermute | solution.py:25
  49.8 2.6 %collective-permute-start.13 = (bf16[4,8704]{1,0:T(4,128)(2,1)S(1)}, bf16[4,8704]{1,0:T(4,128)(2,1)S(1)}, u32[]{:S(2)}, u32[]{:S(2)}) collective-permute-start(bf16[4,8704]{1,0:T(4,128)(2,1)S(1)} %get-tuple-element.28), channel_id=1, source_target_pairs={{0,6},{1,7},{2,4},{3,5},{4,2},{5,3},{6,0},{7,1},{8,14},{9,15},{10,... | collective-permute-start | bytes 208904 | tf_op jit(solution)/shard_map/ppermute | solution.py:25
  52.3 1.5 %collective-permute-start.14 = (bf16[4,8704]{1,0:T(4,128)(2,1)S(1)}, bf16[4,8704]{1,0:T(4,128)(2,1)S(1)}, u32[]{:S(2)}, u32[]{:S(2)}) collective-permute-start(bf16[4,8704]{1,0:T(4,128)(2,1)S(1)} %get-tuple-element.29), channel_id=1, source_target_pairs={{0,7},{1,6},{2,5},{3,4},{4,3},{5,2},{6,1},{7,0},{8,15},{9,14},{10,... | collective-permute-start | bytes 208904 | tf_op jit(solution)/shard_map/ppermute | solution.py:25
  53.9 2.8 %collective-permute-done.11.rest_3_ = bf16[4,8704]{1,0:T(4,128)(2,1)S(1)} collective-permute-done((bf16[4,8704]{1,0:T(4,128)(2,1)S(1)}, bf16[4,8704]{1,0:T(4,128)(2,1)S(1)}, u32[]{:S(2)}, u32[]{:S(2)}) %collective-permute-start.11) | collective-permute-done | bytes 69664 | tf_op jit(solution)/shard_map/ppermute | solution.py:25
  56.7 3.0 %collective-permute-done.12.rest_4_ = bf16[4,8704]{1,0:T(4,128)(2,1)S(1)} collective-permute-done((bf16[4,8704]{1,0:T(4,128)(2,1)S(1)}, bf16[4,8704]{1,0:T(4,128)(2,1)S(1)}, u32[]{:S(2)}, u32[]{:S(2)}) %collective-permute-start.12) | collective-permute-done | bytes 69664 | tf_op jit(solution)/shard_map/ppermute | solution.py:25
  59.8 1.3 %finish.1 = (bf16[4,8192]{1,0:T(4,128)(2,1)}, bf16[1,8,2048]{2,1,0:T(8,128)(2,1)}) custom-call(s32[2]{0:T(128)S(1)} %pad_add_fusion.place_ref, bf16[4,8704]{1,0:T(4,128)(2,1)S(1)} %collective-permute-done.8.rest_0_, bf16[4,8704]{1,0:T(4,128)(2,1)S(1)} %collective-permute-done.9.rest_1_, bf16[4,8704]{1,0:T(4,128)(2,1)S(1)} %collective-permute-done.10.rest_2_, ...), custom_call_target="tpu_custom_call" | custom-call | tf_op jit(solution)/shard_map/finish/pallas_call | solution.py:401
  (18 shorter events, 0.0 us)
Async XLA Ops:
  0.6 7.4 %collective-permute-start.3 = (bf16[4,8192]{1,0:T(4,128)(2,1)}, bf16[4,8192]{1,0:T(4,128)(2,1)S(1)}, u32[]{:S(2)}, u32[]{:S(2)}) collective-permute-start(bf16[4,8192]{1,0:T(4,128)(2,1)} %refs_0_.1), channel_id=1, source_target_pairs={{0,4},{1,5},{2,6},{3,7},{4,0},{5,1},{6,2},{7,3},{8,12},{9,13},{10,... | collective-permute-start | bytes 196616 | tf_op jit(solution)/shard_map/ppermute | solution.py:25
  4.8 5.6 %collective-permute-start.1 = (bf16[4,8192]{1,0:T(4,128)(2,1)}, bf16[4,8192]{1,0:T(4,128)(2,1)S(1)}, u32[]{:S(2)}, u32[]{:S(2)}) collective-permute-start(bf16[4,8192]{1,0:T(4,128)(2,1)} %refs_0_.1), channel_id=1, source_target_pairs={{0,2},{1,3},{2,0},{3,1},{4,6},{5,7},{6,4},{7,5},{8,10},{9,11},{10,... | collective-permute-start | bytes 196616 | tf_op jit(solution)/shard_map/ppermute | solution.py:25
  6.3 6.3 %collective-permute-start.5 = (bf16[4,8192]{1,0:T(4,128)(2,1)}, bf16[4,8192]{1,0:T(4,128)(2,1)S(1)}, u32[]{:S(2)}, u32[]{:S(2)}) collective-permute-start(bf16[4,8192]{1,0:T(4,128)(2,1)} %refs_0_.1), channel_id=1, source_target_pairs={{0,6},{1,7},{2,4},{3,5},{4,2},{5,3},{6,0},{7,1},{8,14},{9,15},{10,... | collective-permute-start | bytes 196616 | tf_op jit(solution)/shard_map/ppermute | solution.py:25
  6.3 10.8 %collective-permute-start = (bf16[4,8192]{1,0:T(4,128)(2,1)}, bf16[4,8192]{1,0:T(4,128)(2,1)S(1)}, u32[]{:S(2)}, u32[]{:S(2)}) collective-permute-start(bf16[4,8192]{1,0:T(4,128)(2,1)} %refs_0_.1), channel_id=1, source_target_pairs={{0,1},{1,0},{2,3},{3,2},{4,5},{5,4},{6,7},{7,6},{8,9},{9,8},{10,11... | collective-permute-start | bytes 196616 | tf_op jit(solution)/shard_map/ppermute | solution.py:25
  8.1 24.5 %copy-start = (bf16[1024,8192]{1,0:T(8,128)(2,1)S(1)}, bf16[1024,8192]{1,0:T(8,128)(2,1)}, u32[]{:S(2)}) copy-start(bf16[1024,8192]{1,0:T(8,128)(2,1)} %weight.3) | copy-start | bytes 50331652
  8.1 9.1 %collective-permute-start.4 = (bf16[4,8192]{1,0:T(4,128)(2,1)S(1)}, bf16[4,8192]{1,0:T(4,128)(2,1)S(1)}, u32[]{:S(2)}, u32[]{:S(2)}) collective-permute-start(bf16[4,8192]{1,0:T(4,128)(2,1)S(1)} %collective-permute-done.3.refs_4_), channel_id=1, source_target_pairs={{0,1},{1,0},{2,3},{3,2},{4,5},{5,4},{6,7},{7,6},{8,9},{9,8},{10,11... | collective-permute-start | bytes 196616 | tf_op jit(solution)/shard_map/ppermute | solution.py:25
  10.4 6.8 %collective-permute-start.2 = (bf16[4,8192]{1,0:T(4,128)(2,1)S(1)}, bf16[4,8192]{1,0:T(4,128)(2,1)S(1)}, u32[]{:S(2)}, u32[]{:S(2)}) collective-permute-start(bf16[4,8192]{1,0:T(4,128)(2,1)S(1)} %collective-permute-done.1.refs_2_), channel_id=1, source_target_pairs={{0,1},{1,0},{2,3},{3,2},{4,5},{5,4},{6,7},{7,6},{8,9},{9,8},{10,11... | collective-permute-start | bytes 196616 | tf_op jit(solution)/shard_map/ppermute | solution.py:25
  12.6 4.6 %collective-permute-start.6 = (bf16[4,8192]{1,0:T(4,128)(2,1)S(1)}, bf16[4,8192]{1,0:T(4,128)(2,1)S(1)}, u32[]{:S(2)}, u32[]{:S(2)}) collective-permute-start(bf16[4,8192]{1,0:T(4,128)(2,1)S(1)} %collective-permute-done.5.refs_6_), channel_id=1, source_target_pairs={{0,1},{1,0},{2,3},{3,2},{4,5},{5,4},{6,7},{7,6},{8,9},{9,8},{10,11... | collective-permute-start | bytes 196616 | tf_op jit(solution)/shard_map/ppermute | solution.py:25
  14.2 0.7 %copy-start.4 = (s32[64]{0:T(128)S(1)}, s32[64]{0:T(128)}, u32[]{:S(2)}) copy-start(s32[64]{0:T(128)} %param.11) | copy-start | bytes 772
  14.8 0.7 %copy-start.5 = (s32[12]{0:T(128)S(1)}, s32[12]{0:T(128)}, u32[]{:S(2)}) copy-start(s32[12]{0:T(128)} %param.12) | copy-start | bytes 148
  15.5 0.7 %copy-start.6 = (f32[1,128]{1,0:T(1,128)S(1)}, f32[1,128]{1,0:T(1,128)}, u32[]{:S(2)}) copy-start(f32[1,128]{1,0:T(1,128)} %constant.11.clone.freq_ref) | copy-start | bytes 1540
  17.2 2.2 %copy-start.2 = (bf16[1,8192,256]{2,1,0:T(8,128)(2,1)S(1)}, bf16[1,8192,256]{2,1,0:T(8,128)(2,1)}, u32[]{:S(2)}) copy-start(bf16[1,8192,256]{2,1,0:T(8,128)(2,1)} %param.9) | copy-start | bytes 12582916
  19.4 0.8 %copy-start.3 = (bf16[4,8192]{1,0:T(4,128)(2,1)S(1)}, bf16[4,8192]{1,0:T(4,128)(2,1)}, u32[]{:S(2)}) copy-start(bf16[4,8192]{1,0:T(4,128)(2,1)} %refs_0_.1) | copy-start | bytes 196612
  22.1 10.4 %collective-permute-start.7 = (bf16[32,256]{1,0:T(8,128)(2,1)S(1)}, bf16[32,256]{1,0:T(8,128)(2,1)S(1)}, u32[]{:S(2)}, u32[]{:S(2)}) collective-permute-start(bf16[32,256]{1,0:T(8,128)(2,1)S(1)} %get-tuple-element.20.own_ref), channel_id=1, source_target_pairs={{0,8},{8,0},{1,9},{9,1},{2,10},{10,2},{3,11},{11,3},{4,12},{12,4},... | collective-permute-start | bytes 49160 | tf_op jit(solution)/shard_map/ppermute | solution.py:25
  22.2 5.8 %copy-start.1 = (bf16[8192,1024]{1,0:T(8,128)(2,1)S(1)}, bf16[8192,1024]{1,0:T(8,128)(2,1)}, u32[]{:S(2)}) copy-start(bf16[8192,1024]{1,0:T(8,128)(2,1)} %weight.2) | copy-start | bytes 50331652
  42.7 7.1 %collective-permute-start.8 = (bf16[4,8704]{1,0:T(4,128)(2,1)S(1)}, bf16[4,8704]{1,0:T(4,128)(2,1)S(1)}, u32[]{:S(2)}, u32[]{:S(2)}) collective-permute-start(bf16[4,8704]{1,0:T(4,128)(2,1)S(1)} %get-tuple-element.23), channel_id=1, source_target_pairs={{0,1},{1,0},{2,3},{3,2},{4,5},{5,4},{6,7},{7,6},{8,9},{9,8},{10,11... | collective-permute-start | bytes 208904 | tf_op jit(solution)/shard_map/ppermute | solution.py:25
  43.9 8.4 %collective-permute-start.9 = (bf16[4,8704]{1,0:T(4,128)(2,1)S(1)}, bf16[4,8704]{1,0:T(4,128)(2,1)S(1)}, u32[]{:S(2)}, u32[]{:S(2)}) collective-permute-start(bf16[4,8704]{1,0:T(4,128)(2,1)S(1)} %get-tuple-element.24), channel_id=1, source_target_pairs={{0,2},{1,3},{2,0},{3,1},{4,6},{5,7},{6,4},{7,5},{8,10},{9,11},{10,... | collective-permute-start | bytes 208904 | tf_op jit(solution)/shard_map/ppermute | solution.py:25
  43.9 10.0 %collective-permute-start.10 = (bf16[4,8704]{1,0:T(4,128)(2,1)S(1)}, bf16[4,8704]{1,0:T(4,128)(2,1)S(1)}, u32[]{:S(2)}, u32[]{:S(2)}) collective-permute-start(bf16[4,8704]{1,0:T(4,128)(2,1)S(1)} %get-tuple-element.25), channel_id=1, source_target_pairs={{0,3},{1,2},{2,1},{3,0},{4,7},{5,6},{6,5},{7,4},{8,11},{9,10},{10,... | collective-permute-start | bytes 208904 | tf_op jit(solution)/shard_map/ppermute | solution.py:25
  46.2 10.5 %collective-permute-start.11 = (bf16[4,8704]{1,0:T(4,128)(2,1)S(1)}, bf16[4,8704]{1,0:T(4,128)(2,1)S(1)}, u32[]{:S(2)}, u32[]{:S(2)}) collective-permute-start(bf16[4,8704]{1,0:T(4,128)(2,1)S(1)} %get-tuple-element.26), channel_id=1, source_target_pairs={{0,4},{1,5},{2,6},{3,7},{4,0},{5,1},{6,2},{7,3},{8,12},{9,13},{10,... | collective-permute-start | bytes 208904 | tf_op jit(solution)/shard_map/ppermute | solution.py:25
  47.5 12.2 %collective-permute-start.12 = (bf16[4,8704]{1,0:T(4,128)(2,1)S(1)}, bf16[4,8704]{1,0:T(4,128)(2,1)S(1)}, u32[]{:S(2)}, u32[]{:S(2)}) collective-permute-start(bf16[4,8704]{1,0:T(4,128)(2,1)S(1)} %get-tuple-element.27), channel_id=1, source_target_pairs={{0,5},{1,4},{2,7},{3,6},{4,1},{5,0},{6,3},{7,2},{8,13},{9,12},{10,... | collective-permute-start | bytes 208904 | tf_op jit(solution)/shard_map/ppermute | solution.py:25
  49.8 10.0 %collective-permute-start.13 = (bf16[4,8704]{1,0:T(4,128)(2,1)S(1)}, bf16[4,8704]{1,0:T(4,128)(2,1)S(1)}, u32[]{:S(2)}, u32[]{:S(2)}) collective-permute-start(bf16[4,8704]{1,0:T(4,128)(2,1)S(1)} %get-tuple-element.28), channel_id=1, source_target_pairs={{0,6},{1,7},{2,4},{3,5},{4,2},{5,3},{6,0},{7,1},{8,14},{9,15},{10,... | collective-permute-start | bytes 208904 | tf_op jit(solution)/shard_map/ppermute | solution.py:25
  52.3 7.4 %collective-permute-start.14 = (bf16[4,8704]{1,0:T(4,128)(2,1)S(1)}, bf16[4,8704]{1,0:T(4,128)(2,1)S(1)}, u32[]{:S(2)}, u32[]{:S(2)}) collective-permute-start(bf16[4,8704]{1,0:T(4,128)(2,1)S(1)} %get-tuple-element.29), channel_id=1, source_target_pairs={{0,7},{1,6},{2,5},{3,4},{4,3},{5,2},{6,1},{7,0},{8,15},{9,14},{10,... | collective-permute-start | bytes 208904 | tf_op jit(solution)/shard_map/ppermute | solution.py:25
